TPU v7x, 32 devices: a whole 2x2x4 slice. The times are simulated.
32 devices in a mesh: dp: 2 (over y), expert: 4 (over z), ffn: 4 (over x, core).
Axes of the slice: x: 2, y: 2, z: 4, core: 2. Of those that a mesh axis runs over, the one named last changes fastest.
Arguments:
- tokens: bfloat16 [512, 4096], P('expert'), may hold values from -6 to 6
- expert_ids: int32 [512, 2], P('expert'), may hold values from 0 to 3, all different within a row; in each aligned block of 128 rows (0 to 127, 128 to 255, ...) at most 64 rows name the same one
- route_weight: float32 [512, 2], P('expert'), may hold values from 0.05 to 1
- cotangent: bfloat16 [512, 4096], P('expert'), may hold values from -40 to 40
- w_gate: bfloat16 [4, 7168, 4096], P('expert', ('dp', 'ffn')), may hold values from -0.09375 to 0.09375
- w_up: bfloat16 [4, 7168, 4096], P('expert', ('dp', 'ffn')), may hold values from -0.09375 to 0.09375
- w_down: bfloat16 [4, 7168, 4096], P('expert', ('dp', 'ffn')), may hold values from -0.0625 to 0.0625
Outputs:
- layer_out: bfloat16 [512, 4096], P('expert', ('dp', 'ffn'))
- ascent_gate: bfloat16 [4, 7168, 4096], P('expert', ('dp', 'ffn'))
- ascent_up: bfloat16 [4, 7168, 4096], P('expert', ('dp', 'ffn'))
- ascent_down: bfloat16 [4, 7168, 4096], P('expert', ('dp', 'ffn'))
Inputs may be any that keep to these rules, and one draw needn't show every extreme that they name: `expert_ids`: each row names two different experts. Among the rows of one aligned block of 128 no expert is named more than 64 times; in every draw some block names some expert exactly 64 times.
All inputs are finite; a program needn't handle non-finite values.
Results may differ from a plain program's by a relative error of at most 0.017.
Values may be sent and summed in bfloat16 or wider, within the bound.
A program may use at most 128 MiB of HBM per device.

v0:
```python
import jax
import jax.numpy as jnp
from jax import lax
from jax.sharding import PartitionSpec as P

FF = 7168


def silu_parts(pre_act):
    sigmoid_value = jax.nn.sigmoid(pre_act)
    return (pre_act * sigmoid_value, sigmoid_value * (1.0 + pre_act * (1.0 - sigmoid_value)))


def against_rows(left_rows, right_rows):
    return lax.dot_general(
        left_rows, right_rows, (((0,), (0,)), ((), ())), preferred_element_type=jnp.float32
    )


def across_width(left_rows, weight):
    return lax.dot_general(
        left_rows, weight, (((1,), (1,)), ((), ())), preferred_element_type=jnp.float32
    )


def squares_of(matrix):
    return jnp.sum(matrix * matrix)


def on_device(tokens, expert_ids, route_weight, cotangent, w_gate, w_up, w_down):
    tok_rows, feature_width = tokens.shape
    experts = lax.axis_size("expert")
    groups = lax.axis_size(("dp", "ffn"))
    capacity = tok_rows // 2
    slot_count = experts * capacity
    column_width = feature_width // groups
    chosen = expert_ids[:, :, None] == jnp.arange(experts, dtype=jnp.int32)[None, None, :]
    per_token = jnp.sum(chosen.astype(jnp.int32), axis=1)
    earlier = jnp.cumsum(per_token, axis=0) - per_token
    position = jnp.sum(jnp.where(chosen, earlier[:, None, :], 0), axis=2)
    slot_index = expert_ids * capacity + position
    slot_hot = slot_index[:, :, None] == jnp.arange(slot_count, dtype=jnp.int32)[None, None, :]
    hot_all = slot_hot.reshape(tok_rows * 2, slot_count).astype(jnp.bfloat16)
    scaled = (route_weight[:, :, None] * cotangent.astype(jnp.float32)[:, None, :]).astype(
        jnp.bfloat16
    )
    token_slots = against_rows(hot_all, jnp.repeat(tokens, 2, axis=0)).astype(jnp.bfloat16)
    grad_slots = against_rows(hot_all, scaled.reshape(tok_rows * 2, feature_width)).astype(
        jnp.bfloat16
    )
    token_cube = token_slots.reshape(experts, capacity, feature_width)
    grad_cube = grad_slots.reshape(experts, capacity, feature_width)
    column_start = lax.axis_index(("dp", "ffn")) * column_width
    token_part = lax.dynamic_slice_in_dim(token_cube, column_start, column_width, 2)
    grad_part = lax.dynamic_slice_in_dim(grad_cube, column_start, column_width, 2)
    received = (
        lax.all_to_all(token_part, "expert", split_axis=0, concat_axis=0, tiled=True),
        lax.all_to_all(grad_part, "expert", split_axis=0, concat_axis=0, tiled=True),
    )
    slot_rows, slot_grads = (
        lax.all_gather(
            received[0].reshape(slot_count, column_width), ("dp", "ffn"), axis=1, tiled=True
        ),
        lax.all_gather(
            received[1].reshape(slot_count, column_width), ("dp", "ffn"), axis=1, tiled=True
        ),
    )
    gate_weight = w_gate[0]
    up_weight = w_up[0]
    down_weight = w_down[0]
    pre_gate = across_width(slot_rows, gate_weight)
    pre_up = across_width(slot_rows, up_weight)
    activated, derivative = silu_parts(pre_gate)
    hidden = (activated * pre_up).astype(jnp.bfloat16)
    partial_value = jnp.dot(hidden, down_weight, preferred_element_type=jnp.float32)
    grad_down = against_rows(hidden, slot_grads)
    grad_hidden = across_width(slot_grads, down_weight)
    delta_gate = (grad_hidden * pre_up * derivative).astype(jnp.bfloat16)
    delta_up = (grad_hidden * activated).astype(jnp.bfloat16)
    grad_gate = against_rows(delta_gate, slot_rows)
    grad_up = against_rows(delta_up, slot_rows)
    sum_squares = lax.psum(
        squares_of(grad_gate) + squares_of(grad_up) + squares_of(grad_down), ("dp", "expert", "ffn")
    )
    summed = lax.psum_scatter(
        partial_value.astype(jnp.bfloat16), ("dp", "ffn"), scatter_dimension=1, tiled=True
    )
    summed = summed.reshape(experts, capacity, column_width)
    returned_rows = lax.all_to_all(
        summed, "expert", split_axis=0, concat_axis=0, tiled=True
    ).reshape(slot_count, column_width)
    picked = jnp.dot(hot_all, returned_rows, preferred_element_type=jnp.float32).reshape(
        tok_rows, 2, column_width
    )
    layer_out = jnp.sum(route_weight[:, :, None] * picked, axis=1).astype(jnp.bfloat16)
    inv_rms = lax.rsqrt(sum_squares / (3.0 * experts * FF * feature_width) + 1e-06)
    return (
        layer_out,
        (grad_gate * inv_rms).astype(jnp.bfloat16)[None],
        (grad_up * inv_rms).astype(jnp.bfloat16)[None],
        (grad_down * inv_rms).astype(jnp.bfloat16)[None],
    )


def solution(mesh):
    return jax.shard_map(
        on_device,
        mesh=mesh,
        in_specs=(
            P("expert", None),
            P("expert", None),
            P("expert", None),
            P("expert", None),
            P("expert", ("dp", "ffn"), None),
            P("expert", ("dp", "ffn"), None),
            P("expert", ("dp", "ffn"), None),
        ),
        out_specs=(
            P("expert", ("dp", "ffn")),
            P("expert", ("dp", "ffn"), None),
            P("expert", ("dp", "ffn"), None),
            P("expert", ("dp", "ffn"), None),
        ),
        check_vma=False,
    )
```

profile of v0, /device:TPU:0, one launch (start us, length us, event | category | flops | bytes accessed | tf_op | source)
XLA Modules:
  0.0 195.2 jit_solution(6774078264472581371)
XLA Ops:
  7.2 0.0 copy-start
  7.2 0.0 copy-start.4
  7.2 0.0 copy-start.6
  7.2 0.0 all-gather.3.cloned.1.call-start
  7.3 0.8 convert_reduce_fusion
  8.1 0.1 copy.12
  8.2 0.2 reduce_window_sum.11
  8.4 0.1 copy.14
  8.4 0.7 select_reduce_fusion
  9.2 0.7 multiply_add_fusion
  9.8 0.0 copy-done
  9.8 0.7 fusion.14
  10.6 15.1 %all_to_all.15 = bf16[4,64,512]{2,1,0:T(8,128)(2,1)} all-to-all(bf16[4,64,512]{2,1,0:T(8,128)(2,1)S(1)} %constant_dynamic-slice_fusion), channel_id=1, replica_groups=mesh['dp'=2,'expert'=4,'ffn'=4] {'expert'}, dimensions={0} | all-to-all | bytes 524288 | tf_op jit(solution)/shard_map/all_to_all | solution.py:57
  25.7 0.0 all-gather.3.cloned.1.call-update
  25.8 0.0 all-gather.5.cloned.1.call-start
  25.8 0.0 copy-done.4
  25.8 0.2 convert_element_type.45
  26.0 0.0 copy-done.6
  26.0 0.8 fusion.15
  26.9 11.1 %all_to_all.16 = bf16[4,64,512]{2,1,0:T(8,128)(2,1)} all-to-all(bf16[4,64,512]{2,1,0:T(8,128)(2,1)S(1)} %constant_dynamic-slice_fusion.1), channel_id=1, replica_groups=mesh['dp'=2,'expert'=4,'ffn'=4] {'expert'}, dimensions={0} | all-to-all | bytes 524288 | tf_op jit(solution)/shard_map/all_to_all | solution.py:58
  38.0 0.0 all-gather.5.cloned.1.call-update
  38.0 0.2 reduce-scatter.2.cloned.1.call-start
  38.3 14.9 %all-gather.3.cloned.1.call-done = bf16[256,4096]{1,0:T(8,128)(2,1)} async-done(((bf16[256,512]{1,0:T(8,128)(2,1)}), bf16[256,4096]{1,0:T(8,128)(2,1)}) %all-gather.3.cloned.1.call-update) | async-done | bytes 2097168 | tf_op jit(solution)/shard_map/all_gather | solution.py:61
  53.1 0.0 copy-start.2
  53.1 0.0 slice-start
  53.1 6.2 %fusion.9 = f32[256,896]{1,0:T(8,128)S(1)} fusion(bf16[256,4096]{1,0:T(8,128)(2,1)} %all-gather.3.cloned.1.call-done, bf16[1,896,4096]{2,1,0:T(8,128)(2,1)} %param.11), kind=kOutput, calls=%fused_computation.15 | convolution fusion | flops 1879048192 | bytes 10354688 | tf_op jit(solution)/shard_map/dot_general | solution.py:21
  59.3 0.0 copy-done.2
  59.4 0.0 slice-start.1
  59.4 6.7 %multiply_convert_fusion.7 = (bf16[256,896]{1,0:T(8,128)(2,1)S(1)}, f32[256,896]{1,0:T(8,128)}) fusion(f32[256,896]{1,0:T(8,128)S(1)} %fusion.9, bf16[256,4096]{1,0:T(8,128)(2,1)S(1)} %copy-done.2, bf16[1,896,4096]{2,1,0:T(8,128)(2,1)} %param.12), kind=kOutput, calls=%fused_computation.30 | convolution fusion | flops 1880424448 | bytes 11730944 | tf_op jit(solution)/shard_map/dot_general | solution.py:21
  66.1 0.0 copy-start.5
  66.1 0.8 copy-done.5
  66.9 0.0 slice-done
  66.9 0.0 slice-done.1
  66.9 3.7 %fusion.11 = bf16[256,4096]{1,0:T(8,128)(2,1)} fusion(bf16[256,896]{1,0:T(8,128)(2,1)S(1)} %get-tuple-element.4, bf16[1,896,4096]{2,1,0:T(8,128)(2,1)S(1)} %bitcast.56), kind=kOutput, calls=%fused_computation.19 | convolution fusion | flops 1880096768 | bytes 9895936 | tf_op jit(solution)/shard_map/dot_general | solution.py:75
  70.5 0.0 reduce-scatter.2.cloned.1.call-update
  70.5 12.6 %all-gather.5.cloned.1.call-done = bf16[256,4096]{1,0:T(8,128)(2,1)} async-done(((bf16[256,512]{1,0:T(8,128)(2,1)}), bf16[256,4096]{1,0:T(8,128)(2,1)}) %all-gather.5.cloned.1.call-update) | async-done | bytes 2097168 | tf_op jit(solution)/shard_map/all_gather | solution.py:64
  83.1 6.1 %fusion.3 = f32[256,896]{1,0:T(8,128)S(1)} fusion(bf16[256,4096]{1,0:T(8,128)(2,1)} %all-gather.5.cloned.1.call-done, bf16[1,896,4096]{2,1,0:T(8,128)(2,1)} %param.13), kind=kOutput, calls=%fused_computation.9 | convolution fusion | flops 1879048192 | bytes 10354688 | tf_op jit(solution)/shard_map/dot_general | solution.py:21
  89.3 0.0 copy-done.3
  89.3 8.6 %multiply_reduce_fusion.2 = (f32[]{:T(128)}, f32[896,4096]{1,0:T(8,128)}) fusion(bf16[256,4096]{1,0:T(8,128)(2,1)S(1)} %copy-done.2, f32[256,896]{1,0:T(8,128)S(1)} %fusion.9, f32[256,896]{1,0:T(8,128)S(1)} %fusion.3, f32[256,896]{1,0:T(8,128)S(1)} %copy-done.3), kind=kOutput, calls=%fused_computation.5 | convolution fusion | flops 1888681984 | bytes 19529732 | tf_op jit(solution)/shard_map/dot_general | solution.py:15
  97.9 8.3 %multiply_reduce_fusion.1 = (f32[]{:T(128)}, f32[896,4096]{1,0:T(8,128)}) fusion(bf16[256,4096]{1,0:T(8,128)(2,1)S(1)} %copy-done.2, f32[256,896]{1,0:T(8,128)S(1)} %fusion.3, f32[256,896]{1,0:T(8,128)S(1)} %fusion.9), kind=kOutput, calls=%fused_computation.4 | convolution fusion | flops 1887764480 | bytes 18612228 | tf_op jit(solution)/shard_map/dot_general | solution.py:15
  107.5 9.8 %multiply_reduce_fusion = (f32[]{:T(128)}, f32[896,4096]{1,0:T(8,128)}) fusion(bf16[256,896]{1,0:T(8,128)(2,1)} %copy-done.5, bf16[256,4096]{1,0:T(8,128)(2,1)} %all-gather.5.cloned.1.call-done), kind=kOutput, calls=%fused_computation.3 | convolution fusion | flops 1886388224 | bytes 17235972 | tf_op jit(solution)/shard_map/dot_general | solution.py:15
  118.0 39.8 %psum.7 = f32[]{:T(128)} all-reduce(f32[]{:T(128)S(6)} %add.35), channel_id=1, replica_groups=mesh['dp'=2,'expert'=4,'ffn'=4] {'dp','expert','ffn'}, use_global_device_ids=true, to_apply=%region_8.9 | all-reduce | flops 1 | bytes 8 | tf_op jit(solution)/shard_map/psum | solution.py:82
  158.4 15.5 %fusion = (bf16[1,896,4096]{2,1,0:T(8,128)(2,1)}, bf16[1,896,4096]{2,1,0:T(8,128)(2,1)}) fusion(f32[896,4096]{1,0:T(8,128)} %get-tuple-element.7, f32[]{:T(128)S(6)} %rsqrt.3, f32[896,4096]{1,0:T(8,128)} %get-tuple-element.9), kind=kLoop, calls=%fused_computation.6 | loop fusion | flops 14680064 | bytes 44040196 | tf_op jit(solution)/shard_map/broadcast_in_dim | solution.py:99
  173.9 3.6 %all-to-all-start.1 = ((bf16[4,64,512]{2,1,0:T(8,128)(2,1)}), bf16[4,64,512]{2,1,0:T(8,128)(2,1)S(1)}, u32[]{:S(2)}, u32[]{:S(2)}) async-start(bf16[4,64,512]{2,1,0:T(8,128)(2,1)} %bitcast.53), calls=%async_computation.2 | async-start | bytes 524288 | tf_op jit(solution)/shard_map/all_to_all | solution.py:89
  177.5 10.3 %fusion.2 = bf16[1,896,4096]{2,1,0:T(8,128)(2,1)} fusion(f32[896,4096]{1,0:T(8,128)} %get-tuple-element.11, f32[]{:T(128)S(6)} %rsqrt.3), kind=kLoop, calls=%fused_computation.8 | loop fusion | flops 7340032 | bytes 22020100 | tf_op jit(solution)/shard_map/broadcast_in_dim | solution.py:101
  187.7 0.0 all-to-all-done.1
  187.7 0.9 fusion.18
  188.7 0.0 copy-done.1
  (7 shorter events, 0.1 us)
Async XLA Ops:
  7.2 2.7 %copy-start = (bf16[128,4096]{1,0:T(8,128)(2,1)S(1)}, bf16[128,4096]{1,0:T(8,128)(2,1)}, u32[]{:S(2)}) copy-start(bf16[128,4096]{1,0:T(8,128)(2,1)} %param.7) | copy-start | bytes 3145732
  7.2 18.6 %copy-start.4 = (bf16[128,4096]{1,0:T(8,128)(2,1)S(1)}, bf16[128,4096]{1,0:T(8,128)(2,1)}, u32[]{:S(2)}) copy-start(bf16[128,4096]{1,0:T(8,128)(2,1)} %param.10) | copy-start | bytes 3145732
  7.2 18.8 %copy-start.6 = (f32[128,2]{0,1:T(2,128)S(1)}, f32[128,2]{0,1:T(2,128)}, u32[]{:S(2)}) copy-start(f32[128,2]{0,1:T(2,128)} %param.9) | copy-start | bytes 3076
  7.2 45.9 %all-gather.3.cloned.1.call-start = ((), (), s32[]{:S(2)}) async-start(), calls=%async_computation.4 | async-start | bytes 2359296 | tf_op jit(solution)/shard_map/all_gather | solution.py:61
  25.8 57.4 %all-gather.5.cloned.1.call-start = ((), (), s32[]{:S(2)}) async-start(), calls=%async_computation.6 | async-start | bytes 2359296 | tf_op jit(solution)/shard_map/all_gather | solution.py:64
  38.0 135.9 %reduce-scatter.2.cloned.1.call-start = ((), (), s32[]{:S(2)}) async-start(), calls=%async_computation.5 | async-start | bytes 2359296 | tf_op jit(solution)/shard_map/reduce_scatter | solution.py:85
  53.1 6.2 %copy-start.2 = (bf16[256,4096]{1,0:T(8,128)(2,1)S(1)}, bf16[256,4096]{1,0:T(8,128)(2,1)}, u32[]{:S(2)}) copy-start(bf16[256,4096]{1,0:T(8,128)(2,1)} %all-gather.3.cloned.1.call-done) | copy-start | bytes 6291460
  53.1 13.7 %slice-start = ((s8[7340032]{0:T(1024)(128)(4,1)}), s8[4194304]{0:T(1024)(128)(4,1)S(1)}, s32[]{:S(2)}) async-start(s8[7340032]{0:T(1024)(128)(4,1)} %bitcast.55), calls=%async_computation.7 | async-start | bytes 8388608
  59.4 7.5 %slice-start.1 = ((s8[7340032]{0:T(1024)(128)(4,1)}), s8[3145728]{0:T(1024)(128)(4,1)S(1)}, s32[]{:S(2)}) async-start(s8[7340032]{0:T(1024)(128)(4,1)} %bitcast.55), calls=%async_computation.8 | async-start | bytes 6291456
  66.1 0.8 copy-start.5
  83.1 6.2 %copy-start.3 = (f32[256,896]{1,0:T(8,128)S(1)}, f32[256,896]{1,0:T(8,128)}, u32[]{:S(2)}) copy-start(f32[256,896]{1,0:T(8,128)} %get-tuple-element.5) | copy-start | bytes 2752516
  173.9 13.8 %all-to-all-start.1 = ((bf16[4,64,512]{2,1,0:T(8,128)(2,1)}), bf16[4,64,512]{2,1,0:T(8,128)(2,1)S(1)}, u32[]{:S(2)}, u32[]{:S(2)}) async-start(bf16[4,64,512]{2,1,0:T(8,128)(2,1)} %bitcast.53), calls=%async_computation.2 | async-start | bytes 524288 | tf_op jit(solution)/shard_map/all_to_all | solution.py:89
  177.5 11.2 %copy-start.1 = (bf16[128,4096]{1,0:T(8,128)(2,1)S(1)}, bf16[128,4096]{1,0:T(8,128)(2,1)}, u32[]{:S(2)}) copy-start(bf16[128,4096]{1,0:T(8,128)(2,1)} %param.7) | copy-start | bytes 3145732
Sparse Core Ops, SparseCore 0:
  25.9 27.1 all-gather.2
  55.0 28.0 all-gather.4
  87.0 41.6 reduce-scatter.1
where the time goes:
time: 196 us; the launch traced here: 195 us
  blocking collectives  66 us (34%)
  matrix products  51.9 us (26%)
  other arithmetic  28.4 us (14%)
  waiting for transfers between devices  27.5 us (14%)
  between operations  16.5 us (8%)
  starting transfers between devices  3.85 us (2%)
    psum x1, blocking collectives, on_device(): lax.psum(squares_of(grad_gate) + squares_of(grad_up) + squares_of(grad_do...  39.8 us
    dot_general x5, matrix products, against_rows(): lax.dot_general(left_rows, right_rows, (((0,), (0,)), ((), ())), preferre...  28.3 us
    dot_general x3, matrix products, across_width(): lax.dot_general(left_rows, weight, (((1,), (1,)), ((), ())), preferred_el...  19.1 us
    broadcast_in_dim x1, other arithmetic, on_device(): (grad_gate * inv_rms).astype(jnp.bfloat16)[None]  15.5 us
    all_to_all x1, blocking collectives, on_device(): lax.all_to_all(token_part, 'expert', split_axis=0, concat_axis=0, tiled=T...  15.1 us
    all_gather x1, waiting for transfers between devices, on_device(): lax.all_gather(received[0].reshape(slot_count, column_width), ('dp', 'ffn...  14.9 us
    all_gather x1, waiting for transfers between devices, on_device(): lax.all_gather(received[1].reshape(slot_count, column_width), ('dp', 'ffn...  12.6 us
    all_to_all x1, blocking collectives, on_device(): lax.all_to_all(grad_part, 'expert', split_axis=0, concat_axis=0, tiled=True)  11.1 us
  transfers between devices with their start and end apart: 4, of which 2 were waited for; matrix products, arithmetic and copies ran while one was open for 39% of the time, Pallas kernels for 0%

commit v1 on v0

--- a/solution.py
+++ b/solution.py
@@ -61,8 +61,8 @@
         lax.all_gather(
             received[0].reshape(slot_count, column_width), ("dp", "ffn"), axis=1, tiled=True
         ),
-        lax.all_gather(
-            received[1].reshape(slot_count, column_width), ("dp", "ffn"), axis=1, tiled=True
+        jnp.concatenate(
+            lax.all_gather(received[1].reshape(slot_count, column_width), ("dp", "ffn")), axis=1
         ),
     )
     gate_weight = w_gate[0]

time: 196 us -> 199 us (1.015)
  local copies, waits for them, and re-layouts: 1.04 us -> 4.07 us
    all_gather x0 -> x1, local copies, waits for them, and re-layouts: none -> 3.03 us  [on_device(): lax.all_gather(received[1].reshape(slot_count, column_width), ('dp', 'ffn'))]
  transfers between devices with their start and end apart: 4 -> 4, of which waited for: 2 -> 2; matrix products, arithmetic and copies ran while one was open for 39% -> 40% of each run, Pallas kernels for 0% -> 0%
where the time goes in v1:
time: 199 us; the launch traced here: 198 us
  blocking collectives  65.6 us (33%)
  matrix products  52.6 us (26%)
  other arithmetic  28.4 us (14%)
  waiting for transfers between devices  27.1 us (14%)
  between operations  16.6 us (8%)
  local copies, waits for them, and re-layouts  4.07 us (2%)
  starting transfers between devices  3.67 us (2%)
    psum x1, blocking collectives, on_device(): lax.psum(squares_of(grad_gate) + squares_of(grad_up) + squares_of(grad_do...  39.4 us
    dot_general x5, matrix products, against_rows(): lax.dot_general(left_rows, right_rows, (((0,), (0,)), ((), ())), preferre...  29.2 us
    dot_general x3, matrix products, across_width(): lax.dot_general(left_rows, weight, (((1,), (1,)), ((), ())), preferred_el...  18.8 us
    broadcast_in_dim x1, other arithmetic, on_device(): (grad_gate * inv_rms).astype(jnp.bfloat16)[None]  15.5 us
    all_to_all x1, blocking collectives, on_device(): lax.all_to_all(token_part, 'expert', split_axis=0, concat_axis=0, tiled=T...  15.1 us
    all_gather x1, waiting for transfers between devices, on_device(): lax.all_gather(received[0].reshape(slot_count, column_width), ('dp', 'ffn...  15 us
    all_gather x1, waiting for transfers between devices, on_device(): lax.all_gather(received[1].reshape(slot_count, column_width), ('dp', 'ffn'))  12 us
    all_to_all x1, blocking collectives, on_device(): lax.all_to_all(grad_part, 'expert', split_axis=0, concat_axis=0, tiled=True)  11.1 us
  transfers between devices with their start and end apart: 4, of which 2 were waited for; matrix products, arithmetic and copies ran while one was open for 40% of the time, Pallas kernels for 0%

profile of v1, /device:TPU:0, one launch (start us, length us, event | category | flops | bytes accessed | tf_op | source)
XLA Modules:
  0.0 198.0 jit_solution(4676071659224278645)
XLA Ops:
  7.2 0.0 copy-start
  7.2 0.0 copy-start.5
  7.2 0.0 copy-start.7
  7.2 0.0 all-gather.3.cloned.1.call-start
  7.3 0.8 convert_reduce_fusion
  8.1 0.1 copy.18
  8.2 0.2 reduce_window_sum.11
  8.4 0.1 copy.20
  8.4 0.7 select_reduce_fusion
  9.2 0.7 multiply_add_fusion
  9.8 0.0 copy-done
  9.8 0.7 fusion.14
  10.6 15.1 %all_to_all.15 = bf16[4,64,512]{2,1,0:T(8,128)(2,1)} all-to-all(bf16[4,64,512]{2,1,0:T(8,128)(2,1)S(1)} %constant_dynamic-slice_fusion), channel_id=1, replica_groups=mesh['dp'=2,'expert'=4,'ffn'=4] {'expert'}, dimensions={0} | all-to-all | bytes 524288 | tf_op jit(solution)/shard_map/all_to_all | solution.py:57
  25.7 0.0 all-gather.3.cloned.1.call-update
  25.8 0.0 all-gather.5.cloned.1.call-start
  25.8 0.0 copy-done.5
  25.8 0.2 convert_element_type.45
  26.0 0.0 copy-done.7
  26.0 0.8 fusion.15
  26.9 11.1 %all_to_all.16 = bf16[4,64,512]{2,1,0:T(8,128)(2,1)} all-to-all(bf16[4,64,512]{2,1,0:T(8,128)(2,1)S(1)} %constant_dynamic-slice_fusion.1), channel_id=1, replica_groups=mesh['dp'=2,'expert'=4,'ffn'=4] {'expert'}, dimensions={0} | all-to-all | bytes 524288 | tf_op jit(solution)/shard_map/all_to_all | solution.py:58
  38.0 0.0 all-gather.5.cloned.1.call-update
  38.0 0.0 reduce-scatter.2.cloned.1.call-start
  38.1 15.0 %all-gather.3.cloned.1.call-done = bf16[256,4096]{1,0:T(8,128)(2,1)} async-done(((bf16[256,512]{1,0:T(8,128)(2,1)}), bf16[256,4096]{1,0:T(8,128)(2,1)}) %all-gather.3.cloned.1.call-update) | async-done | bytes 2097168 | tf_op jit(solution)/shard_map/all_gather | solution.py:61
  53.1 6.2 %fusion.9 = f32[256,896]{1,0:T(8,128)S(1)} fusion(bf16[256,4096]{1,0:T(8,128)(2,1)} %all-gather.3.cloned.1.call-done, bf16[1,896,4096]{2,1,0:T(8,128)(2,1)} %param.11), kind=kOutput, calls=%fused_computation.15 | convolution fusion | flops 1879048192 | bytes 10354688 | tf_op jit(solution)/shard_map/dot_general | solution.py:21
  59.3 0.0 copy-done.2
  59.4 0.0 slice-start.1
  59.4 7.0 %multiply_convert_fusion.7 = (bf16[256,896]{1,0:T(8,128)(2,1)S(1)}, f32[256,896]{1,0:T(8,128)}) fusion(f32[256,896]{1,0:T(8,128)S(1)} %fusion.9, bf16[256,4096]{1,0:T(8,128)(2,1)S(1)} %copy-done.2, bf16[1,896,4096]{2,1,0:T(8,128)(2,1)} %param.12), kind=kOutput, calls=%fused_computation.30 | convolution fusion | flops 1880424448 | bytes 11730944 | tf_op jit(solution)/shard_map/dot_general | solution.py:21
  66.3 0.8 copy-done.6
  67.1 0.0 slice-done
  67.1 0.0 slice-done.1
  67.1 3.7 %fusion.11 = bf16[256,4096]{1,0:T(8,128)(2,1)} fusion(bf16[256,896]{1,0:T(8,128)(2,1)S(1)} %get-tuple-element.4, bf16[1,896,4096]{2,1,0:T(8,128)(2,1)S(1)} %bitcast.61), kind=kOutput, calls=%fused_computation.19 | convolution fusion | flops 1880096768 | bytes 9895936 | tf_op jit(solution)/shard_map/dot_general | solution.py:75
  70.8 0.0 reduce-scatter.2.cloned.1.call-update
  70.8 12.0 %all-gather.5.cloned.1.call-done = bf16[8,256,512]{2,1,0:T(8,128)(2,1)} async-done(((bf16[1,256,512]{2,1,0:T(8,128)(2,1)}), bf16[8,256,512]{2,1,0:T(8,128)(2,1)}) %all-gather.5.cloned.1.call-update) | async-done | bytes 2097168 | tf_op jit(solution)/shard_map/all_gather | solution.py:65
  82.8 3.0 %copy.21 = bf16[8,256,512]{1,2,0:T(8,128)(2,1)S(1)} copy(bf16[8,256,512]{2,1,0:T(8,128)(2,1)} %all-gather.5.cloned.1.call-done) | data formatting | bytes 4194304 | tf_op jit(solution)/shard_map/all_gather | solution.py:65
  85.8 0.0 copy-start.3
  85.9 0.0 copy-start.4
  85.9 5.6 %fusion.3 = f32[256,896]{1,0:T(8,128)S(1)} fusion(bf16[256,4096]{0,1:T(8,128)(2,1)S(1)} %bitcast.52, bf16[1,896,4096]{2,1,0:T(8,128)(2,1)} %param.13), kind=kOutput, calls=%fused_computation.9 | convolution fusion | flops 1879048192 | bytes 10354688 | tf_op jit(solution)/shard_map/dot_general | solution.py:21
  91.5 0.0 copy-done.3
  91.5 0.0 copy-done.4
  91.5 8.6 %multiply_reduce_fusion.2 = (f32[]{:T(128)}, f32[896,4096]{1,0:T(8,128)}) fusion(bf16[256,4096]{1,0:T(8,128)(2,1)S(1)} %copy-done.3, f32[256,896]{1,0:T(8,128)S(1)} %fusion.9, f32[256,896]{1,0:T(8,128)S(1)} %fusion.3, f32[256,896]{1,0:T(8,128)S(1)} %copy-done.4), kind=kOutput, calls=%fused_computation.5 | convolution fusion | flops 1888681984 | bytes 19529732 | tf_op jit(solution)/shard_map/dot_general | solution.py:15
  100.1 8.0 %multiply_reduce_fusion.1 = (f32[]{:T(128)}, f32[896,4096]{1,0:T(8,128)}) fusion(bf16[256,4096]{1,0:T(8,128)(2,1)S(1)} %copy-done.3, f32[256,896]{1,0:T(8,128)S(1)} %fusion.3, f32[256,896]{1,0:T(8,128)S(1)} %fusion.9), kind=kOutput, calls=%fused_computation.4 | convolution fusion | flops 1887764480 | bytes 18612228 | tf_op jit(solution)/shard_map/dot_general | solution.py:15
  109.5 11.0 %multiply_reduce_fusion = (f32[]{:T(128)}, f32[896,4096]{1,0:T(8,128)}) fusion(bf16[256,896]{1,0:T(8,128)(2,1)} %copy-done.6, bf16[256,4096]{0,1:T(8,128)(2,1)S(1)} %bitcast.53), kind=kOutput, calls=%fused_computation.3 | convolution fusion | flops 1886388224 | bytes 17235972 | tf_op jit(solution)/shard_map/dot_general | solution.py:15
  121.1 39.4 %psum.7 = f32[]{:T(128)} all-reduce(f32[]{:T(128)S(6)} %add.35), channel_id=1, replica_groups=mesh['dp'=2,'expert'=4,'ffn'=4] {'dp','expert','ffn'}, use_global_device_ids=true, to_apply=%region_8.9 | all-reduce | flops 1 | bytes 8 | tf_op jit(solution)/shard_map/psum | solution.py:82
  161.2 15.5 %fusion = (bf16[1,896,4096]{2,1,0:T(8,128)(2,1)}, bf16[1,896,4096]{2,1,0:T(8,128)(2,1)}) fusion(f32[896,4096]{1,0:T(8,128)} %get-tuple-element.7, f32[]{:T(128)S(6)} %rsqrt.3, f32[896,4096]{1,0:T(8,128)} %get-tuple-element.9), kind=kLoop, calls=%fused_computation.6 | loop fusion | flops 14680064 | bytes 44040196 | tf_op jit(solution)/shard_map/broadcast_in_dim | solution.py:99
  176.7 3.5 %all-to-all-start.1 = ((bf16[4,64,512]{2,1,0:T(8,128)(2,1)}), bf16[4,64,512]{2,1,0:T(8,128)(2,1)S(1)}, u32[]{:S(2)}, u32[]{:S(2)}) async-start(bf16[4,64,512]{2,1,0:T(8,128)(2,1)} %bitcast.58), calls=%async_computation.2 | async-start | bytes 524288 | tf_op jit(solution)/shard_map/all_to_all | solution.py:89
  180.3 10.3 %fusion.2 = bf16[1,896,4096]{2,1,0:T(8,128)(2,1)} fusion(f32[896,4096]{1,0:T(8,128)} %get-tuple-element.11, f32[]{:T(128)S(6)} %rsqrt.3), kind=kLoop, calls=%fused_computation.8 | loop fusion | flops 7340032 | bytes 22020100 | tf_op jit(solution)/shard_map/broadcast_in_dim | solution.py:101
  190.5 0.0 all-to-all-done.1
  190.5 0.9 fusion.18
  (10 shorter events, 0.1 us)
Async XLA Ops:
  7.2 2.7 %copy-start = (bf16[128,4096]{1,0:T(8,128)(2,1)S(1)}, bf16[128,4096]{1,0:T(8,128)(2,1)}, u32[]{:S(2)}) copy-start(bf16[128,4096]{1,0:T(8,128)(2,1)} %param.7) | copy-start | bytes 3145732
  7.2 18.6 %copy-start.5 = (bf16[128,4096]{1,0:T(8,128)(2,1)S(1)}, bf16[128,4096]{1,0:T(8,128)(2,1)}, u32[]{:S(2)}) copy-start(bf16[128,4096]{1,0:T(8,128)(2,1)} %param.10) | copy-start | bytes 3145732
  7.2 18.8 %copy-start.7 = (f32[128,2]{0,1:T(2,128)S(1)}, f32[128,2]{0,1:T(2,128)}, u32[]{:S(2)}) copy-start(f32[128,2]{0,1:T(2,128)} %param.9) | copy-start | bytes 3076
  7.2 45.9 %all-gather.3.cloned.1.call-start = ((), (), s32[]{:S(2)}) async-start(), calls=%async_computation.4 | async-start | bytes 2359296 | tf_op jit(solution)/shard_map/all_gather | solution.py:61
  25.8 57.1 %all-gather.5.cloned.1.call-start = ((), (), s32[]{:S(2)}) async-start(), calls=%async_computation.6 | async-start | bytes 2359296 | tf_op jit(solution)/shard_map/all_gather | solution.py:65
  38.0 138.7 %reduce-scatter.2.cloned.1.call-start = ((), (), s32[]{:S(2)}) async-start(), calls=%async_computation.5 | async-start | bytes 2359296 | tf_op jit(solution)/shard_map/reduce_scatter | solution.py:85
  53.1 6.2 %copy-start.2 = (bf16[256,4096]{1,0:T(8,128)(2,1)S(1)}, bf16[256,4096]{1,0:T(8,128)(2,1)}, u32[]{:S(2)}) copy-start(bf16[256,4096]{1,0:T(8,128)(2,1)} %all-gather.3.cloned.1.call-done) | copy-start | bytes 6291460
  53.1 14.0 %slice-start = ((s8[7340032]{0:T(1024)(128)(4,1)}), s8[4194304]{0:T(1024)(128)(4,1)S(1)}, s32[]{:S(2)}) async-start(s8[7340032]{0:T(1024)(128)(4,1)} %bitcast.60), calls=%async_computation.7 | async-start | bytes 8388608
  59.4 7.7 %slice-start.1 = ((s8[7340032]{0:T(1024)(128)(4,1)}), s8[3145728]{0:T(1024)(128)(4,1)S(1)}, s32[]{:S(2)}) async-start(s8[7340032]{0:T(1024)(128)(4,1)} %bitcast.60), calls=%async_computation.8 | async-start | bytes 6291456
  66.3 0.8 copy-start.6
  85.8 5.6 %copy-start.3 = (bf16[256,4096]{1,0:T(8,128)(2,1)S(1)}, bf16[256,4096]{1,0:T(8,128)(2,1)}, u32[]{:S(2)}) copy-start(bf16[256,4096]{1,0:T(8,128)(2,1)} %all-gather.3.cloned.1.call-done) | copy-start | bytes 6291460
  85.9 5.6 %copy-start.4 = (f32[256,896]{1,0:T(8,128)S(1)}, f32[256,896]{1,0:T(8,128)}, u32[]{:S(2)}) copy-start(f32[256,896]{1,0:T(8,128)} %get-tuple-element.5) | copy-start | bytes 2752516
  176.7 13.8 %all-to-all-start.1 = ((bf16[4,64,512]{2,1,0:T(8,128)(2,1)}), bf16[4,64,512]{2,1,0:T(8,128)(2,1)S(1)}, u32[]{:S(2)}, u32[]{:S(2)}) async-start(bf16[4,64,512]{2,1,0:T(8,128)(2,1)} %bitcast.58), calls=%async_computation.2 | async-start | bytes 524288 | tf_op jit(solution)/shard_map/all_to_all | solution.py:89
  180.3 11.2 %copy-start.1 = (bf16[128,4096]{1,0:T(8,128)(2,1)S(1)}, bf16[128,4096]{1,0:T(8,128)(2,1)}, u32[]{:S(2)}) copy-start(bf16[128,4096]{1,0:T(8,128)(2,1)} %param.7) | copy-start | bytes 3145732
Sparse Core Ops, SparseCore 0:
  25.9 27.1 all-gather.2
  55.0 27.7 all-gather.4
  86.7 41.1 reduce-scatter.1
